TPU v7x, 32 devices: a whole 2x2x4 slice. The times are simulated.
32 devices in a mesh: ep: 8 (over z, x), etp: 4 (over y, core).
Axes of the slice: x: 2, y: 2, z: 4, core: 2. Of those that a mesh axis runs over, the one named last changes fastest.
Arguments:
- tokens: bfloat16 [1024, 4096], P('ep', 'etp'), may hold values from -6 to 6
- expert_ids: int32 [1024, 8], P('ep'), may hold values from 0 to 15, all different within a row; in each aligned block of 128 rows (0 to 127, 128 to 255, ...) at most 96 rows name the same one
- gate_prob: float32 [1024, 8], P('ep'), may hold values from 0.05 to 1
- gate_weight: bfloat16 [16, 4096, 1536], P('ep', None, 'etp'), may hold values from -0.09375 to 0.09375
- up_weight: bfloat16 [16, 4096, 1536], P('ep', None, 'etp'), may hold values from -0.09375 to 0.09375
- down_weight: bfloat16 [16, 1536, 4096], P('ep', 'etp'), may hold values from -0.15625 to 0.15625
Outputs:
- mixed: bfloat16 [1024, 4096], P('ep', 'etp')
Inputs may be any that keep to these rules, and one draw needn't show every extreme that they name: `expert_ids`: each row names 8 different experts. Within each aligned block of 128 rows (one token group) no expert is named more than 96 times, and in every draw some expert is named exactly 96 times in some block.
All inputs are finite; a program needn't handle non-finite values.
Results may differ from a plain program's by a relative error of at most 0.012.
Values may be sent and summed in bfloat16 or wider, within the bound.
A program may use at most 128 MiB of HBM per device.

v0:
```python
from functools import partial

import jax
import jax.numpy as jnp
from jax import lax
from jax.sharding import PartitionSpec as P


def add_features(totals, portion, offset, w_gate, w_up):
    return (
        jnp.dot(portion, w_gate, preferred_element_type=jnp.float32),
        jnp.dot(portion, w_up, preferred_element_type=jnp.float32),
    )


def body(tokens, expert_ids, gate_prob, gate_weight, up_weight, down_weight):
    groups = lax.axis_size("ep")
    local_experts = gate_weight.shape[0]
    experts = local_experts * groups
    tok_rows = expert_ids.shape[0]
    fanout = expert_ids.shape[1]
    capacity = max(2, 3 * tok_rows * fanout // (2 * experts))
    flat_ids = expert_ids.reshape(-1)
    onehot = (flat_ids[:, None] == jnp.arange(experts, dtype=jnp.int32)[None, :]).astype(jnp.int32)
    position = jnp.sum((jnp.cumsum(onehot, axis=0) - onehot) * onehot, axis=1)
    slot_index = flat_ids * capacity + position
    owners = jnp.arange(tok_rows * fanout, dtype=jnp.int32) // fanout
    source = jnp.full((experts * capacity,), tok_rows, jnp.int32).at[slot_index].set(owners)
    padded = jnp.concatenate([tokens, jnp.zeros((1, tokens.shape[1]), tokens.dtype)], axis=0)
    outgoing = padded[source].reshape(groups, local_experts, capacity, tokens.shape[1])
    arrived = lax.all_to_all(outgoing, "ep", split_axis=0, concat_axis=2, tiled=True)
    partials = []
    for member in range(local_experts):
        expert_rows = arrived[0, member]
        starting = jnp.zeros((expert_rows.shape[0], gate_weight.shape[2]), jnp.float32)
        folder = partial(add_features, w_gate=gate_weight[member], w_up=up_weight[member])
        gate_sum, up_sum = folder(
            (starting, starting),
            lax.all_gather(expert_rows, "etp", axis=1, tiled=True),
            jnp.int32(0),
        )
        hidden = (jax.nn.silu(gate_sum) * up_sum).astype(jnp.bfloat16)
        partials.append(jnp.dot(hidden, down_weight[member], preferred_element_type=jnp.float32))
    partial_all = jnp.stack(partials).reshape(local_experts, groups, capacity, down_weight.shape[2])
    combine_scale = gate_prob.reshape(tok_rows, fanout, 1)
    summed = lax.psum_scatter(
        partial_all.astype(jnp.bfloat16), "etp", scatter_dimension=3, tiled=True
    ).astype(jnp.float32)
    returned = lax.all_to_all(
        summed.astype(jnp.bfloat16), "ep", split_axis=1, concat_axis=0, tiled=True
    ).astype(summed.dtype)
    picked = returned.reshape(experts * capacity, -1)[slot_index].reshape(tok_rows, fanout, -1)
    mixed = jnp.sum(picked * combine_scale, axis=1).astype(jnp.bfloat16)
    return mixed


def solution(mesh):
    in_specs = (
        P("ep", "etp"),
        P("ep", None),
        P("ep", None),
        P("ep", None, "etp"),
        P("ep", None, "etp"),
        P("ep", "etp", None),
    )
    out_specs = P("ep", "etp")
    return jax.shard_map(body, mesh=mesh, in_specs=in_specs, out_specs=out_specs, check_vma=False)
```

profile of v0, /device:TPU:0, one launch (start us, length us, event | category | flops | bytes accessed | tf_op | source)
XLA Modules:
  0.0 419.7 jit_solution(9803007199391855178)
XLA Ops:
  6.5 0.0 all-gather.5.cloned.1.call-start
  6.5 0.8 copy.19
  7.3 0.1 eq.29
  7.4 0.1 eq.25
  7.5 0.7 broadcast_multiply_fusion
  8.2 4.5 %reduce-window.6 = s32[16,8,128]{2,1,0:T(8,128)S(1)} reduce-window(s32[16,8,128]{2,1,0:T(8,128)S(1)} %fusion.46, s32[]{:T(128)} %constant.32.clone.1), window={size=1x1x128 pad=0_0x0_0x127_0}, to_apply=%region_0.0 | reduce-window | flops 2080768 | bytes 131076 | tf_op jit(solution)/shard_map/reduce-window
  12.7 0.1 slice.44
  12.8 0.1 copy.21
  13.0 0.1 copy.22
  13.1 0.1 broadcast_add_fusion
  13.1 0.1 copy.18
  13.2 0.1 mul.42
  13.4 4.3 %scatter_custom_fusion = s32[1536]{0:T(1024)S(1)} fusion(s32[1024]{0:T(1024)S(1)} %bitcast.98, s32[1024]{0:T(1024)S(1)} %add_select_fusion, s32[]{:T(128)} %constant.30.clone.1), kind=kCustom, calls=%fused_computation.52 | custom fusion | bytes 6148 | tf_op jit(solution)/shard_map/scatter | solution.py:28
  17.7 1.0 concatenate.5
  18.7 5.1 %gather_fusion = bf16[1536,1024]{1,0:T(8,128)(2,1)S(1)} fusion(bf16[129,1024]{1,0:T(8,128)(2,1)S(1)} %concatenate.5, s32[2048]{0:T(1024)S(1)} %pad_clamp_fusion), kind=kCustom, calls=%fused_computation | custom fusion | bytes 6297600 | tf_op jit(solution)/shard_map/gather | solution.py:30
  23.8 77.8 %all_to_all.27 = bf16[8,2,96,1024]{3,2,1,0:T(8,128)(2,1)S(1)} all-to-all(bf16[8,2,96,1024]{3,2,1,0:T(8,128)(2,1)S(1)} %bitcast.92), channel_id=1, replica_groups=mesh['ep'=8,'etp'=4] {'ep'}, dimensions={0} | all-to-all | bytes 6291456 | tf_op jit(solution)/shard_map/all_to_all | solution.py:31
  101.6 0.4 copy.23
  102.0 1.9 fusion.52
  104.0 0.0 all-gather.5.cloned.1.call-update
  104.0 0.0 all-gather.7.cloned.1.call-start
  104.0 0.7 all-gather.7.cloned.1.call-update
  104.7 0.2 reduce-scatter.2.cloned.1.call-start
  105.0 44.6 %all-gather.5.cloned.1.call-done = bf16[1,1,768,4096]{3,2,1,0:T(8,128)(2,1)} async-done(((bf16[1,1,768,1024]{3,2,1,0:T(8,128)(2,1)}), bf16[1,1,768,4096]{3,2,1,0:T(8,128)(2,1)}) %all-gather.5.cloned.1.call-update) | async-done | bytes 6291472 | tf_op jit(solution)/shard_map/all_gather | solution.py:39
  149.5 6.6 %fusion.6 = f32[768,384]{1,0:T(8,128)S(1)} fusion(bf16[1,1,768,4096]{3,2,1,0:T(8,128)(2,1)} %all-gather.5.cloned.1.call-done, bf16[2,4096,384]{2,1,0:T(8,128)(2,1)} %param.9), kind=kOutput, calls=%fused_computation.12 | convolution fusion | flops 2415919104 | bytes 10616832 | tf_op jit(solution)/shard_map/dot_general | solution.py:11
  156.1 0.0 copy-done.1
  156.1 0.0 slice-start.3
  156.1 5.9 %fusion.38 = bf16[768,384]{1,0:T(8,128)(2,1)S(1)} fusion(bf16[2,4096,384]{2,1,0:T(8,128)(2,1)} %param.10, bf16[1,1,768,4096]{3,2,1,0:T(8,128)(2,1)S(1)} %copy-done.1, f32[768,384]{1,0:T(8,128)S(1)} %fusion.6), kind=kOutput, calls=%fused_computation.34 | convolution fusion | flops 2417688576 | bytes 11206656 | tf_op jit(solution)/shard_map/dot_general | solution.py:12
  162.0 0.0 slice-done.2
  162.0 0.0 slice-done.3
  162.0 5.4 %fusion.8 = bf16[1,8,96,4096]{3,2,1,0:T(8,128)(2,1)} fusion(bf16[8,96,384]{2,1,0:T(8,128)(2,1)S(1)} %bitcast.104, bf16[2,384,4096]{2,1,0:T(8,128)(2,1)S(1)} %bitcast.101), kind=kOutput, calls=%fused_computation.14 | convolution fusion | flops 2419064832 | bytes 10027008 | tf_op jit(solution)/shard_map/dot_general | solution.py:43
  167.4 30.1 %all-gather.7.cloned.1.call-done = bf16[1,1,768,4096]{3,2,1,0:T(8,128)(2,1)} async-done(((bf16[1,1,768,1024]{3,2,1,0:T(8,128)(2,1)}), bf16[1,1,768,4096]{3,2,1,0:T(8,128)(2,1)}) %all-gather.7.cloned.1.call-update) | async-done | bytes 6291472 | tf_op jit(solution)/shard_map/all_gather | solution.py:39
  197.5 6.6 %fusion.2 = f32[768,384]{1,0:T(8,128)S(1)} fusion(bf16[1,1,768,4096]{3,2,1,0:T(8,128)(2,1)} %all-gather.7.cloned.1.call-done, bf16[2,4096,384]{2,1,0:T(8,128)(2,1)} %param.9), kind=kOutput, calls=%fused_computation.8 | convolution fusion | flops 2415919104 | bytes 10616832 | tf_op jit(solution)/shard_map/dot_general | solution.py:11
  204.1 0.0 copy-done.2
  204.1 0.0 slice-start.5
  204.1 0.0 slice-start.1
  204.1 5.7 %fusion.33 = bf16[768,384]{1,0:T(8,128)(2,1)S(1)} fusion(bf16[2,4096,384]{2,1,0:T(8,128)(2,1)} %param.10, bf16[1,1,768,4096]{3,2,1,0:T(8,128)(2,1)S(1)} %copy-done.2, f32[768,384]{1,0:T(8,128)S(1)} %fusion.2), kind=kOutput, calls=%fused_computation.33 | convolution fusion | flops 2417688576 | bytes 11206656 | tf_op jit(solution)/shard_map/dot_general | solution.py:12
  209.8 0.0 slice-done.4
  209.9 3.6 fusion.9
  213.5 5.3 %pad_maximum_fusion = bf16[2,8,96,4096]{3,2,1,0:T(8,128)(2,1)} fusion(bf16[1,8,96,4096]{3,2,1,0:T(8,128)(2,1)S(1)} %fusion.9, bf16[1,8,96,4096]{3,2,1,0:T(8,128)(2,1)S(1)} %bitcast.94), kind=kLoop, calls=%fused_computation.3 | loop fusion | flops 6291456 | bytes 25165824 | tf_op jit(solution)/shard_map/stack | solution.py:44
  218.8 0.0 reduce-scatter.2.cloned.1.call-update
  218.8 97.3 %reduce-scatter.2.cloned.1.call-done = bf16[2,8,96,1024]{3,2,1,0:T(8,128)(2,1)} async-done(((bf16[2,8,96,4096]{3,2,1,0:T(8,128)(2,1)}), bf16[2,8,96,1024]{3,2,1,0:T(8,128)(2,1)}) %reduce-scatter.2.cloned.1.call-update) | async-done | bytes 3145744 | tf_op jit(solution)/shard_map/reduce_scatter | solution.py:46
  316.1 3.9 copy.24
  320.1 5.6 %all-to-all-start.1 = ((bf16[2,8,96,1024]{3,2,0,1:T(8,128)(2,1)}), bf16[2,8,96,1024]{3,2,0,1:T(8,128)(2,1)S(1)}, u32[]{:S(2)}, u32[]{:S(2)}) async-start(bf16[2,8,96,1024]{3,2,0,1:T(8,128)(2,1)} %copy.24), calls=%async_computation.2 | async-start | bytes 6291456 | tf_op jit(solution)/shard_map/all_to_all | solution.py:49
  325.7 0.1 copy.25
  325.8 70.4 %all-to-all-done.1 = bf16[2,8,96,1024]{3,2,0,1:T(8,128)(2,1)S(1)} async-done(((bf16[2,8,96,1024]{3,2,0,1:T(8,128)(2,1)}), bf16[2,8,96,1024]{3,2,0,1:T(8,128)(2,1)S(1)}, u32[]{:S(2)}, u32[]{:S(2)}) %all-to-all-start.1) | async-done | bytes 3145760 | tf_op jit(solution)/shard_map/all_to_all | solution.py:49
  396.3 3.4 bitcast_convert_fusion
  399.7 9.3 %gather_fusion.1 = f32[1024,1024]{1,0:T(8,128)} fusion(f32[1536,1024]{1,0:T(8,128)} %bitcast.90, s32[1024]{0:T(1024)S(1)} %broadcast_clamp_fusion), kind=kCustom, calls=%fused_computation.1 | custom fusion | bytes 8392704 | tf_op jit(solution)/shard_map/gather | solution.py:52
  409.0 4.2 fusion.10
  (22 shorter events, 0.1 us)
Async XLA Ops:
  6.5 143.0 %all-gather.5.cloned.1.call-start = ((), (), s32[]{:S(2)}) async-start(), calls=%async_computation.4 | async-start | bytes 7864320 | tf_op jit(solution)/shard_map/all_gather | solution.py:39
  104.0 93.5 %all-gather.7.cloned.1.call-start = ((), (), s32[]{:S(2)}) async-start(), calls=%async_computation.5 | async-start | bytes 7864320 | tf_op jit(solution)/shard_map/all_gather | solution.py:39
  104.7 211.4 %reduce-scatter.2.cloned.1.call-start = ((), (), s32[]{:S(2)}) async-start(), calls=%async_computation.3 | async-start | bytes 15728640 | tf_op jit(solution)/shard_map/reduce_scatter | solution.py:46
  149.5 6.6 %copy-start.1 = (bf16[1,1,768,4096]{3,2,1,0:T(8,128)(2,1)S(1)}, bf16[1,1,768,4096]{3,2,1,0:T(8,128)(2,1)}, u32[]{:S(2)}) copy-start(bf16[1,1,768,4096]{3,2,1,0:T(8,128)(2,1)} %all-gather.5.cloned.1.call-done) | copy-start | bytes 18874372
  149.5 12.5 %slice-start.2 = ((s8[6291456]{0:T(1024)(128)(4,1)}), s8[4194304]{0:T(1024)(128)(4,1)S(1)}, s32[]{:S(2)}) async-start(s8[6291456]{0:T(1024)(128)(4,1)} %bitcast.100), calls=%async_computation.8 | async-start | bytes 8388608
  156.1 5.9 %slice-start.3 = ((s8[6291456]{0:T(1024)(128)(4,1)}), s8[2097152]{0:T(1024)(128)(4,1)S(1)}, s32[]{:S(2)}) async-start(s8[6291456]{0:T(1024)(128)(4,1)} %bitcast.100), calls=%async_computation.9 | async-start | bytes 4194304
  197.5 6.6 %copy-start.2 = (bf16[1,1,768,4096]{3,2,1,0:T(8,128)(2,1)S(1)}, bf16[1,1,768,4096]{3,2,1,0:T(8,128)(2,1)}, u32[]{:S(2)}) copy-start(bf16[1,1,768,4096]{3,2,1,0:T(8,128)(2,1)} %all-gather.7.cloned.1.call-done) | copy-start | bytes 18874372
  197.5 12.4 %slice-start.4 = ((s8[6291456]{0:T(1024)(128)(4,1)}), s8[4194304]{0:T(1024)(128)(4,1)S(1)}, s32[]{:S(2)}) async-start(s8[6291456]{0:T(1024)(128)(4,1)} %bitcast.102), calls=%async_computation.10 | async-start | bytes 8388608
  197.5 16.0 %slice-start = ((s8[6291456]{0:T(1024)(128)(4,1)}), s8[4194304]{0:T(1024)(128)(4,1)S(1)}, s32[]{:S(2)}) async-start(s8[6291456]{0:T(1024)(128)(4,1)} %bitcast.93), calls=%async_computation.6 | async-start | bytes 8388608
  204.1 5.8 %slice-start.5 = ((s8[6291456]{0:T(1024)(128)(4,1)}), s8[2097152]{0:T(1024)(128)(4,1)S(1)}, s32[]{:S(2)}) async-start(s8[6291456]{0:T(1024)(128)(4,1)} %bitcast.102), calls=%async_computation.11 | async-start | bytes 4194304
  204.1 9.4 %slice-start.1 = ((s8[6291456]{0:T(1024)(128)(4,1)}), s8[2097152]{0:T(1024)(128)(4,1)S(1)}, s32[]{:S(2)}) async-start(s8[6291456]{0:T(1024)(128)(4,1)} %bitcast.93), calls=%async_computation.7 | async-start | bytes 4194304
  320.1 5.6 %copy-start = (f32[128,8]{0,1:T(8,128)S(1)}, f32[128,8]{0,1:T(8,128)}, u32[]{:S(2)}) copy-start(f32[128,8]{0,1:T(8,128)} %param.8) | copy-start | bytes 12292
  320.1 76.2 %all-to-all-start.1 = ((bf16[2,8,96,1024]{3,2,0,1:T(8,128)(2,1)}), bf16[2,8,96,1024]{3,2,0,1:T(8,128)(2,1)S(1)}, u32[]{:S(2)}, u32[]{:S(2)}) async-start(bf16[2,8,96,1024]{3,2,0,1:T(8,128)(2,1)} %copy.24), calls=%async_computation.2 | async-start | bytes 6291456 | tf_op jit(solution)/shard_map/all_to_all | solution.py:49
Sparse Core Ops, SparseCore 0:
  104.1 45.3 all-gather.4
  151.1 46.3 all-gather.6
  219.0 97.1 reduce-scatter.1
where the time goes:
time: 420 us
  waiting for transfers between devices  243 us (58%)
  blocking collectives  77.8 us (19%)
  matrix products  33.8 us (8%)
  local copies, waits for them, and re-layouts  27.5 us (7%)
  other arithmetic  18.3 us (4%)
  between operations  13.3 us (3%)
  starting transfers between devices  5.9 us (1%)
    reduce_scatter x1, waiting for transfers between devices, body(): lax.psum_scatter(partial_all.astype(jnp.bfloat16), 'etp', scatter_dimensi...  97.3 us
    all_to_all x1, blocking collectives, body(): lax.all_to_all(outgoing, 'ep', split_axis=0, concat_axis=2, tiled=True)  77.8 us
    all_gather x2, waiting for transfers between devices, body(): lax.all_gather(expert_rows, 'etp', axis=1, tiled=True)  74.6 us
    all_to_all x1, waiting for transfers between devices, body(): lax.all_to_all(summed.astype(jnp.bfloat16), 'ep', split_axis=1, concat_ax...  70.4 us
    dot_general x2, matrix products, add_features(): jnp.dot(portion, w_gate, preferred_element_type=jnp.float32)  13.1 us
    dot_general x2, matrix products, add_features(): jnp.dot(portion, w_up, preferred_element_type=jnp.float32)  11.6 us
    gather x1, local copies, waits for them, and re-layouts, body(): returned.reshape(experts * capacity, -1)[slot_index]  9.27 us
    dot_general x2, matrix products, body(): jnp.dot(hidden, down_weight[member], preferred_element_type=jnp.float32)  9 us
  transfers between devices with their start and end apart: 4, of which 4 were waited for; matrix products, arithmetic and copies ran while one was open for 4% of the time, Pallas kernels for 0%

commit v1 on v0

v1 whole, which is shorter than its diff:
```python
import functools

import jax
import jax.numpy as jnp
from jax import lax
from jax.experimental import pallas as pl
from jax.experimental.pallas import tpu as pltpu
from jax.sharding import PartitionSpec as P

MESH = pl.DeviceIdType.MESH
VMEM_BUDGET = 16 << 20


def place(sizes):
    ep, etp = lax.axis_index("ep"), lax.axis_index("etp")
    return (ep // 2, ep % 2, etp // 2, etp % 2)


def moved(here, sizes, rel):
    return tuple((h + r) % n if r else h for h, n, r in zip(here, sizes, rel))


def device(at):
    z, x, y, c = at
    return (z * 2 + x, y * 2 + c)


def barrier(here, sizes, rels):
    sem = pltpu.get_barrier_semaphore()
    for rel in rels:
        pl.semaphore_signal(sem, inc=1, device_id=device(moved(here, sizes, rel)), device_id_type=MESH)
    pl.semaphore_wait(sem, len(rels))


def gather_kernel(sizes, x_ref, w_ref, out_ref, w_out_ref, send_sem, recv_sem, w_send, w_recv, own_sem):
    nz = sizes[0]
    rows, cols = x_ref.shape
    half = rows // 2
    here = place(sizes)
    z_rels = [(d, 0, 0, 0) for d in range(1, nz)]
    ep_rels = [(d, e, 0, 0) for d in range(nz) for e in range(2) if d or e]
    barrier(here, sizes, ep_rels + [(0, 0, 1, 0), (0, 0, 0, 1)])

    def number(rel):
        return ((rel[0] * 2 + rel[1]) * 2 + rel[2]) * 2 + rel[3]

    def slot(h, rel):
        group, member = device(moved(here, sizes, rel))
        return out_ref.at[pl.ds(pl.multiple_of(group * rows + h * half, half), half),
                          pl.ds(pl.multiple_of(member * cols, cols), cols)]

    sends = []

    def send(h, rel, step):
        lands = tuple((r - s) % n for r, s, n in zip(rel, step, sizes))
        src = slot(h, rel) if any(rel) else x_ref.at[pl.ds(h * half, half), :]
        copy = pltpu.make_async_remote_copy(
            src_ref=src, dst_ref=slot(h, rel), send_sem=send_sem.at[len(sends)],
            recv_sem=recv_sem.at[h, number(lands)],
            device_id=device(moved(here, sizes, step)), device_id_type=MESH)
        copy.start()
        sends.append(copy)

    def arrive(h, rel):
        ref = slot(h, rel)
        pltpu.make_async_copy(ref, ref, recv_sem.at[h, number(rel)]).wait()

    first = {0: (0, 1, 0, 0), 1: (0, 0, 1, 0)}
    second = {0: (0, 0, 1, 0), 1: (0, 1, 0, 0)}
    other = (0, 0, 0, 1)

    own = pltpu.make_async_copy(
        x_ref, out_ref.at[pl.ds(pl.multiple_of(device(here)[0] * rows, rows), rows),
                          pl.ds(pl.multiple_of(device(here)[1] * cols, cols), cols)], own_sem)
    own.start()
    for step in z_rels:
        for h in range(2):
            send(h, (0, 0, 0, 0), step)
    for h in range(2):
        send(h, (0, 0, 0, 0), first[h])
    for h in range(2):
        send(h, (0, 0, 0, 0), second[h])
    for h in range(2):
        send(h, (0, 0, 0, 0), other)
    w_sends = []
    me = device(here)[0]
    for i, rel in enumerate(ep_rels):
        back = tuple((-r) % n for r, n in zip(rel, sizes))
        copy = pltpu.make_async_remote_copy(
            src_ref=w_ref, dst_ref=w_out_ref.at[me], send_sem=w_send.at[i],
            recv_sem=w_recv.at[ep_rels.index(back)],
            device_id=device(moved(here, sizes, rel)), device_id_type=MESH)
        copy.start()
        w_sends.append(copy)
    w_own = pltpu.make_async_copy(w_ref, w_out_ref.at[me], w_recv.at[len(ep_rels)])
    w_own.start()
    order = sorted(range(1, nz), key=lambda d: min(d, nz - d))
    for d in order:
        for h in range(2):
            arrive(h, (d, 0, 0, 0))
            send(h, (d, 0, 0, 0), first[h])
            send(h, (d, 0, 0, 0), second[h])
            send(h, (d, 0, 0, 0), other)
    for d in [0] + order:
        for h in range(2):
            rel = (d,) + first[h][1:]
            arrive(h, rel)
            send(h, rel, second[h])
            send(h, rel, other)
    for d in [0] + order:
        for h in range(2):
            rel = (d,) + second[h][1:]
            arrive(h, rel)
            send(h, rel, other)
    for d in [0] + order:
        for h in range(2):
            rel = (d, 1, 1, 0)
            arrive(h, rel)
            send(h, rel, other)
    for d in range(nz):
        for e in range(2):
            for f in range(2):
                for h in range(2):
                    arrive(h, (d, e, f, 1))
    for i in range(len(ep_rels)):
        w_sends[i].wait_send()
        ref = w_out_ref.at[0]
        pltpu.make_async_copy(ref, ref, w_recv.at[i]).wait()
    for copy in sends:
        copy.wait_send()
    own.wait()
    w_own.wait()


def gather(sizes, x, w):
    groups, parts = sizes[0] * sizes[1], sizes[2] * sizes[3]
    rows, cols = x.shape
    n_send = 2 * (sizes[0] - 1 + sizes[0] + 2 * sizes[0] + 4 * sizes[0])
    return pl.pallas_call(
        functools.partial(gather_kernel, sizes),
        out_shape=(jax.ShapeDtypeStruct((groups * rows, parts * cols), x.dtype),
                   jax.ShapeDtypeStruct((groups,) + w.shape, w.dtype)),
        in_specs=[pl.BlockSpec(memory_space=pltpu.VMEM)] * 2,
        out_specs=(pl.BlockSpec(memory_space=pl.ANY), pl.BlockSpec(memory_space=pltpu.VMEM)),
        scratch_shapes=[
            pltpu.SemaphoreType.DMA((n_send,)),
            pltpu.SemaphoreType.DMA((2, groups * parts)),
            pltpu.SemaphoreType.DMA((groups - 1,)),
            pltpu.SemaphoreType.DMA((groups,)),
            pltpu.SemaphoreType.DMA,
        ],
        compiler_params=pltpu.CompilerParams(collective_id=0, has_side_effects=True, vmem_limit_bytes=16 << 20),
        name="gather_tokens",
    )(x, w)


def scatter_kernel(sizes, p_ref, out_ref, buf_c, buf_1, buf_2, buf_z, send_sem, recv_c, recv_1, recv_2, recv_z):
    nz = sizes[0]
    rows, cols = out_ref.shape
    half = rows // 2
    here = place(sizes)
    barrier(here, sizes, [(d, 0, 0, 0) for d in range(1, nz)] + [(0, 1, 0, 0), (0, 0, 1, 0), (0, 0, 0, 1)])
    axis = ((0, 1, 0, 0), (0, 0, 1, 0))
    first = {0: axis[1], 1: axis[0]}
    second = {0: axis[0], 1: axis[1]}
    sends = []

    def local(h, rel):
        group, member = device(moved(here, sizes, rel))
        return p_ref.at[pl.ds(pl.multiple_of(group * rows + h * half, half), half),
                        pl.ds(pl.multiple_of(member * cols, cols), cols)]

    def rel_of(h, a, b, d):
        e, f = (b, a) if h == 0 else (a, b)
        return (d, e, f)

    def send(src, dst, recv, step):
        copy = pltpu.make_async_remote_copy(
            src_ref=src, dst_ref=dst, send_sem=send_sem.at[len(sends)], recv_sem=recv,
            device_id=device(moved(here, sizes, step)), device_id_type=MESH)
        copy.start()
        sends.append(copy)

    def arrive(ref, sem):
        pltpu.make_async_copy(ref, ref, sem).wait()

    def add(dst, *srcs):
        chunk = 16

        @pl.loop(0, half // chunk)
        def _(i):
            at = pl.ds(pl.multiple_of(i * chunk, chunk), chunk)
            total = srcs[0][at, :].astype(jnp.float32)
            for src in srcs[1:]:
                total = total + src[at, :].astype(jnp.float32)
            dst[at, :] = total.astype(dst.dtype)

    zs = list(range(1, nz)) + [0]
    for a, b in ((1, 1), (1, 0), (0, 1), (0, 0)):
        for d in zs:
            for h in range(2):
                send(local(h, rel_of(h, a, b, d) + (1,)), buf_c.at[h, a, b, d], recv_c.at[h, a, b, d], (0, 0, 0, 1))
    for b in (1, 0):
        for d in zs:
            for h in range(2):
                piece = buf_c.at[h, 1, b, d]
                arrive(piece, recv_c.at[h, 1, b, d])
                add(piece, piece, local(h, rel_of(h, 1, b, d) + (0,)))
                send(piece, buf_1.at[h, b, d], recv_1.at[h, b, d], first[h])
    for d in zs:
        for h in range(2):
            piece = buf_c.at[h, 0, 1, d]
            arrive(piece, recv_c.at[h, 0, 1, d])
            arrive(buf_1.at[h, 1, d], recv_1.at[h, 1, d])
            add(piece, piece, local(h, rel_of(h, 0, 1, d) + (0,)), buf_1.at[h, 1, d])
            send(piece, buf_2.at[h, d], recv_2.at[h, d], second[h])
    for d in zs:
        for h in range(2):
            piece = buf_c.at[h, 0, 0, d]
            arrive(piece, recv_c.at[h, 0, 0, d])
            arrive(buf_1.at[h, 0, d], recv_1.at[h, 0, d])
            arrive(buf_2.at[h, d], recv_2.at[h, d])
            srcs = (piece, local(h, rel_of(h, 0, 0, d) + (0,)), buf_1.at[h, 0, d], buf_2.at[h, d])
            if d:
                add(piece, *srcs)
                send(piece, buf_z.at[h, nz - d - 1], recv_z.at[h, nz - d - 1], (d, 0, 0, 0))
            else:
                for k in range(nz - 1):
                    arrive(buf_z.at[h, k], recv_z.at[h, k])
                add(out_ref.at[pl.ds(h * half, half), :], *srcs, *[buf_z.at[h, k] for k in range(nz - 1)])
    for copy in sends:
        copy.wait_send()


def scatter(sizes, p):
    nz = sizes[0]
    groups, parts = nz * 2, sizes[2] * sizes[3]
    rows, cols = p.shape[0] // groups, p.shape[1] // parts
    half = rows // 2
    n_send = 2 * (4 * nz + 2 * nz + nz + nz - 1)
    return pl.pallas_call(
        functools.partial(scatter_kernel, sizes),
        out_shape=jax.ShapeDtypeStruct((rows, cols), p.dtype),
        in_specs=[pl.BlockSpec(memory_space=pltpu.VMEM)],
        out_specs=pl.BlockSpec(memory_space=pltpu.VMEM),
        scratch_shapes=[
            pltpu.VMEM((2, 2, 2, nz, half, cols), p.dtype),
            pltpu.VMEM((2, 2, nz, half, cols), p.dtype),
            pltpu.VMEM((2, nz, half, cols), p.dtype),
            pltpu.VMEM((2, nz - 1, half, cols), p.dtype),
            pltpu.SemaphoreType.DMA((n_send,)),
            pltpu.SemaphoreType.DMA((2, 2, 2, nz)),
            pltpu.SemaphoreType.DMA((2, 2, nz)),
            pltpu.SemaphoreType.DMA((2, nz)),
            pltpu.SemaphoreType.DMA((2, nz - 1)),
        ],
        compiler_params=pltpu.CompilerParams(collective_id=1, has_side_effects=True, vmem_limit_bytes=40 << 20),
        name="reduce_scatter",
    )(p)


def hidden_kernel(x_ref, w_ref, gate_ref, up_ref, out_ref):
    gate = jnp.dot(x_ref[...], gate_ref[0], preferred_element_type=jnp.float32)
    up = jnp.dot(x_ref[...], up_ref[0], preferred_element_type=jnp.float32)
    out_ref[...] = (jax.nn.silu(gate) * up * w_ref[0]).astype(out_ref.dtype)


def down_kernel(h_ref, down_ref, out_ref):
    out_ref[...] = jnp.dot(h_ref[...], down_ref[...], preferred_element_type=jnp.float32).astype(out_ref.dtype)


def tile_of(total, wanted):
    while total % wanted:
        wanted //= 2
    return wanted


def experts_dense(x, scale, gate_weight, up_weight, down_weight):
    members, width, units = gate_weight.shape
    rows = x.shape[0]
    tile = tile_of(rows, 256)
    hidden = pl.pallas_call(
        hidden_kernel,
        grid=(members, rows // tile),
        out_shape=jax.ShapeDtypeStruct((rows, members * units), x.dtype),
        in_specs=[
            pl.BlockSpec((tile, width), lambda e, m: (m, 0)),
            pl.BlockSpec((1, tile, 1), lambda e, m: (e, m, 0)),
            pl.BlockSpec((1, width, units), lambda e, m: (e, 0, 0)),
            pl.BlockSpec((1, width, units), lambda e, m: (e, 0, 0)),
        ],
        out_specs=pl.BlockSpec((tile, units), lambda e, m: (m, e)),
        compiler_params=pltpu.CompilerParams(vmem_limit_bytes=40 << 20),
        name="hidden",
    )(x, scale, gate_weight, up_weight)
    down = down_weight.reshape(members * units, width)
    tile_n = tile_of(width, 512)
    tile_m = tile_of(rows, 1024)
    return pl.pallas_call(
        down_kernel,
        grid=(rows // tile_m, width // tile_n),
        out_shape=jax.ShapeDtypeStruct((rows, width), x.dtype),
        in_specs=[
            pl.BlockSpec((tile_m, members * units), lambda m, n: (m, 0)),
            pl.BlockSpec((members * units, tile_n), lambda m, n: (0, n)),
        ],
        out_specs=pl.BlockSpec((tile_m, tile_n), lambda m, n: (m, n)),
        compiler_params=pltpu.CompilerParams(vmem_limit_bytes=24 << 20),
        name="down",
    )(hidden, down)


def body(tokens, expert_ids, gate_prob, gate_weight, up_weight, down_weight):
    groups, parts = lax.axis_size("ep"), lax.axis_size("etp")
    members = gate_weight.shape[0]
    numbers = jnp.arange(members * groups, dtype=jnp.int32)
    share = jnp.sum(jnp.where(numbers[:, None, None] == expert_ids[None], gate_prob[None], 0.0), axis=2)
    size = groups * parts * tokens.size * tokens.dtype.itemsize
    kernels = groups % 2 == 0 and groups > 2 and parts == 4 and size <= VMEM_BUDGET
    sizes = (groups // 2, 2, parts // 2, 2)
    if kernels:
        gathered, shares = gather(sizes, tokens, share)
    else:
        gathered = lax.all_gather(lax.all_gather(tokens, "ep", axis=0, tiled=True), "etp", axis=1, tiled=True)
        shares = lax.all_gather(share, "ep", axis=0)
    mine = lax.dynamic_slice_in_dim(shares, lax.axis_index("ep") * members, members, axis=1)
    scale = jnp.transpose(mine, (1, 0, 2)).reshape(members, -1, 1)
    partial_sum = experts_dense(gathered, scale, gate_weight, up_weight, down_weight)
    if kernels:
        return scatter(sizes, partial_sum)
    summed = lax.psum_scatter(partial_sum, "etp", scatter_dimension=1, tiled=True)
    return lax.psum_scatter(summed, "ep", scatter_dimension=0, tiled=True)


def solution(mesh):
    in_specs = (
        P("ep", "etp"),
        P("ep", None),
        P("ep", None),
        P("ep", None, "etp"),
        P("ep", None, "etp"),
        P("ep", "etp", None),
    )
    out_specs = P("ep", "etp")
    return jax.shard_map(body, mesh=mesh, in_specs=in_specs, out_specs=out_specs, check_vma=False)
```

time: 420 us -> 154 us (0.37)
  the two profiles are of different devices: /device:TPU:0 before, /device:TPU:9 now
where the time goes in v1:
time: 154 us; the launch traced here: 153 us
  Pallas kernels  145 us (94%)
  local copies, waits for them, and re-layouts  8.03 us (5%)
    pallas_call x1, Pallas kernels, gather(): pl.pallas_call(functools.partial(gather_kernel, sizes), out_shape=(jax.Sh...  58.5 us
    pallas_call x1, Pallas kernels, scatter(): pl.pallas_call(functools.partial(scatter_kernel, sizes), out_shape=jax.Sh...  55.2 us
    pallas_call x1, Pallas kernels, experts_dense(): pl.pallas_call(hidden_kernel, grid=(members, rows // tile), out_shape=jax...  22 us
    pallas_call x1, Pallas kernels, experts_dense(): pl.pallas_call(down_kernel, grid=(rows // tile_m, width // tile_n), out_s...  8.9 us
    unnamed x9, local copies, waits for them, and re-layouts  7.66 us

profile of v1, /device:TPU:9, one launch (start us, length us, event | category | flops | bytes accessed | tf_op | source)
XLA Modules:
  0.0 153.5 jit_solution(13717538973498480701)
XLA Ops:
  0.0 0.7 select_reduce_fusion.w_ref
  0.7 0.0 copy-start.3
  0.7 0.9 copy-done.3
  1.7 58.5 %gather_tokens.1 = (bf16[1024,4096]{1,0:T(8,128)(2,1)S(1)}, f32[8,16,128]{2,1,0:T(8,128)S(1)}) custom-call(bf16[128,1024]{1,0:T(8,128)(2,1)S(1)} %copy-done.3, f32[16,128]{1,0:T(8,128)S(1)} %select_reduce_fusion.w_ref), custom_call_target="tpu_custom_call" | custom-call | tf_op jit(solution)/shard_map/gather_tokens/pallas_call | solution.py:139
  60.2 0.0 copy-start
  60.2 3.2 %copy-done = bf16[1024,4096]{1,0:T(8,128)(2,1)} copy-done((bf16[1024,4096]{1,0:T(8,128)(2,1)}, bf16[1024,4096]{1,0:T(8,128)(2,1)S(1)}, u32[]{:S(2)}) %copy-start) | copy-done | bytes 8388632
  63.5 0.4 copy.13.w_ref
  63.8 0.0 copy-start.1
  63.8 2.8 %copy-done.1 = bf16[2,4096,384]{2,1,0:T(8,128)(2,1)S(1)} copy-done((bf16[2,4096,384]{2,1,0:T(8,128)(2,1)S(1)}, bf16[2,4096,384]{2,1,0:T(8,128)(2,1)}, u32[]{:S(2)}) %copy-start.1) | copy-done | bytes 6291480
  66.6 0.0 copy-start.2
  66.6 22.0 %hidden.1.h_ref = bf16[1024,768]{1,0:T(8,128)(2,1)S(1)} custom-call(bf16[1024,4096]{1,0:T(8,128)(2,1)} %copy-done, f32[2,1024,1]{2,1,0:T(8,128)S(1)} %copy.13.w_ref, bf16[2,4096,384]{2,1,0:T(8,128)(2,1)S(1)} %copy-done.1, bf16[2,4096,384]{2,1,0:T(8,128)(2,1)} %up_ref.1), custom_call_target="tpu_custom_call" | custom-call | tf_op jit(solution)/shard_map/hidden/pallas_call | solution.py:282
  88.6 0.0 copy-done.2
  88.6 8.9 %down.1.p_ref = bf16[1024,4096]{1,0:T(8,128)(2,1)S(1)} custom-call(bf16[1024,768]{1,0:T(8,128)(2,1)S(1)} %hidden.1.h_ref, bf16[768,4096]{1,0:T(8,128)(2,1)S(1)} %bitcast.5), custom_call_target="tpu_custom_call" | custom-call | tf_op jit(solution)/shard_map/down/pallas_call | solution.py:299
  97.5 55.2 %reduce_scatter.1 = bf16[128,1024]{1,0:T(8,128)(2,1)S(1)} custom-call(bf16[1024,4096]{1,0:T(8,128)(2,1)S(1)} %down.1.p_ref), custom_call_target="tpu_custom_call" | custom-call | tf_op jit(solution)/shard_map/reduce_scatter/pallas_call | solution.py:241
  152.8 0.7 copy.15
  (1 shorter events, 0.0 us)
Async XLA Ops:
  0.7 1.0 copy-start.3
  60.2 3.2 %copy-start = (bf16[1024,4096]{1,0:T(8,128)(2,1)}, bf16[1024,4096]{1,0:T(8,128)(2,1)S(1)}, u32[]{:S(2)}) copy-start(bf16[1024,4096]{1,0:T(8,128)(2,1)S(1)} %get-tuple-element.7.x_ref) | copy-start | bytes 25165828
  63.8 2.8 %copy-start.1 = (bf16[2,4096,384]{2,1,0:T(8,128)(2,1)S(1)}, bf16[2,4096,384]{2,1,0:T(8,128)(2,1)}, u32[]{:S(2)}) copy-start(bf16[2,4096,384]{2,1,0:T(8,128)(2,1)} %gate_ref.1) | copy-start | bytes 18874372
  66.6 22.0 %copy-start.2 = (bf16[2,384,4096]{2,1,0:T(8,128)(2,1)S(1)}, bf16[2,384,4096]{2,1,0:T(8,128)(2,1)}, u32[]{:S(2)}) copy-start(bf16[2,384,4096]{2,1,0:T(8,128)(2,1)} %param.11) | copy-start | bytes 18874372

commit v2 on v1

--- a/solution.py
+++ b/solution.py
@@ -16,8 +16,17 @@
     return (ep // 2, ep % 2, etp // 2, etp % 2)
 
 
+def flip(at, bits):
+    bit = 1
+    while bit <= bits:
+        if bits & bit:
+            at = at + bit - 2 * bit * ((at // bit) % 2)
+        bit *= 2
+    return at
+
+
 def moved(here, sizes, rel):
-    return tuple((h + r) % n if r else h for h, n, r in zip(here, sizes, rel))
+    return tuple(flip(h, r) for h, r in zip(here, rel))
 
 
 def device(at):
@@ -32,7 +41,8 @@
     pl.semaphore_wait(sem, len(rels))
 
 
-def gather_kernel(sizes, x_ref, w_ref, out_ref, w_out_ref, send_sem, recv_sem, w_send, w_recv, own_sem):
+def gather_kernel(sizes, x_ref, w_ref, gate_hbm, up_hbm, hidden_ref, out_ref, w_out_ref,
+                  gate_ref, up_ref, send_sem, recv_sem, w_send, w_recv, own_sem, load_sem):
     nz = sizes[0]
     rows, cols = x_ref.shape
     half = rows // 2
@@ -52,7 +62,7 @@
     sends = []
 
     def send(h, rel, step):
-        lands = tuple((r - s) % n for r, s, n in zip(rel, step, sizes))
+        lands = tuple(r ^ s for r, s in zip(rel, step))
         src = slot(h, rel) if any(rel) else x_ref.at[pl.ds(h * half, half), :]
         copy = pltpu.make_async_remote_copy(
             src_ref=src, dst_ref=slot(h, rel), send_sem=send_sem.at[len(sends)],
@@ -69,89 +79,117 @@
     second = {0: (0, 0, 1, 0), 1: (0, 1, 0, 0)}
     other = (0, 0, 0, 1)
 
+    def pass_on(d):
+        for h in range(2):
+            if d:
+                arrive(h, (d, 0, 0, 0))
+            send(h, (d, 0, 0, 0), first[h])
+            send(h, (d, 0, 0, 0), second[h])
+            send(h, (d, 0, 0, 0), other)
+
+    def pass_second(d):
+        for h in range(2):
+            rel = (d,) + first[h][1:]
+            arrive(h, rel)
+            send(h, rel, second[h])
+            send(h, rel, other)
+
+    def pass_last(d):
+        for h in range(2):
+            for rel in ((d,) + second[h][1:], (d, 1, 1, 0)):
+                arrive(h, rel)
+                send(h, rel, other)
+
     own = pltpu.make_async_copy(
         x_ref, out_ref.at[pl.ds(pl.multiple_of(device(here)[0] * rows, rows), rows),
                           pl.ds(pl.multiple_of(device(here)[1] * cols, cols), cols)], own_sem)
     own.start()
-    for step in z_rels:
+    for step in z_rels[:1]:
         for h in range(2):
             send(h, (0, 0, 0, 0), step)
-    for h in range(2):
-        send(h, (0, 0, 0, 0), first[h])
-    for h in range(2):
-        send(h, (0, 0, 0, 0), second[h])
-    for h in range(2):
-        send(h, (0, 0, 0, 0), other)
+    pass_on(0)
+    for step in z_rels[1:]:
+        for h in range(2):
+            send(h, (0, 0, 0, 0), step)
     w_sends = []
     me = device(here)[0]
     for i, rel in enumerate(ep_rels):
-        back = tuple((-r) % n for r, n in zip(rel, sizes))
         copy = pltpu.make_async_remote_copy(
             src_ref=w_ref, dst_ref=w_out_ref.at[me], send_sem=w_send.at[i],
-            recv_sem=w_recv.at[ep_rels.index(back)],
+            recv_sem=w_recv.at[i],
             device_id=device(moved(here, sizes, rel)), device_id_type=MESH)
         copy.start()
         w_sends.append(copy)
     w_own = pltpu.make_async_copy(w_ref, w_out_ref.at[me], w_recv.at[len(ep_rels)])
     w_own.start()
-    order = sorted(range(1, nz), key=lambda d: min(d, nz - d))
-    for d in order:
-        for h in range(2):
-            arrive(h, (d, 0, 0, 0))
-            send(h, (d, 0, 0, 0), first[h])
-            send(h, (d, 0, 0, 0), second[h])
-            send(h, (d, 0, 0, 0), other)
-    for d in [0] + order:
-        for h in range(2):
-            rel = (d,) + first[h][1:]
-            arrive(h, rel)
-            send(h, rel, second[h])
-            send(h, rel, other)
-    for d in [0] + order:
-        for h in range(2):
-            rel = (d,) + second[h][1:]
-            arrive(h, rel)
-            send(h, rel, other)
-    for d in [0] + order:
-        for h in range(2):
-            rel = (d, 1, 1, 0)
-            arrive(h, rel)
-            send(h, rel, other)
-    for d in range(nz):
+    loads = [pltpu.make_async_copy(gate_hbm, gate_ref, load_sem.at[0]),
+             pltpu.make_async_copy(up_hbm, up_ref, load_sem.at[1])]
+    for load in loads:
+        load.start()
+    members, units = gate_ref.shape[0], gate_ref.shape[2]
+
+    def compute(d):
         for e in range(2):
             for f in range(2):
                 for h in range(2):
                     arrive(h, (d, e, f, 1))
-    for i in range(len(ep_rels)):
-        w_sends[i].wait_send()
-        ref = w_out_ref.at[0]
-        pltpu.make_async_copy(ref, ref, w_recv.at[i]).wait()
+        first_group = flip(here[0], d) * 2
+        at = pl.ds(pl.multiple_of(first_group * rows, 2 * rows), 2 * rows)
+        x = out_ref[at, :]
+        share = w_out_ref[pl.ds(first_group, 2)].reshape(2 * rows, w_ref.shape[1])
+        lane = lax.broadcasted_iota(jnp.int32, share.shape, 1)
+        for m in range(members):
+            scale = jnp.sum(jnp.where(lane == me * members + m, share, 0.0), axis=1, keepdims=True)
+            gate = jnp.dot(x, gate_ref[m], preferred_element_type=jnp.float32)
+            up = jnp.dot(x, up_ref[m], preferred_element_type=jnp.float32)
+            hidden_ref[at, m * units:(m + 1) * units] = (jax.nn.silu(gate) * up * scale).astype(hidden_ref.dtype)
+
+    for d in range(1, nz + 3):
+        if d < nz:
+            pass_on(d)
+        if d <= nz:
+            pass_second(d - 1)
+        if d == 3:
+            for i in range(len(ep_rels)):
+                w_sends[i].wait_send()
+                ref = w_out_ref.at[0]
+                pltpu.make_async_copy(ref, ref, w_recv.at[i]).wait()
+            own.wait()
+            w_own.wait()
+            for load in loads:
+                load.wait()
+        if d >= 3:
+            compute(d - 3)
+        if 2 <= d <= nz + 1:
+            pass_last(d - 2)
     for copy in sends:
         copy.wait_send()
-    own.wait()
-    w_own.wait()
-
-
-def gather(sizes, x, w):
+
+
+def gather(sizes, x, w, gate, up):
     groups, parts = sizes[0] * sizes[1], sizes[2] * sizes[3]
     rows, cols = x.shape
     n_send = 2 * (sizes[0] - 1 + sizes[0] + 2 * sizes[0] + 4 * sizes[0])
     return pl.pallas_call(
         functools.partial(gather_kernel, sizes),
-        out_shape=(jax.ShapeDtypeStruct((groups * rows, parts * cols), x.dtype),
-                   jax.ShapeDtypeStruct((groups,) + w.shape, w.dtype)),
-        in_specs=[pl.BlockSpec(memory_space=pltpu.VMEM)] * 2,
-        out_specs=(pl.BlockSpec(memory_space=pl.ANY), pl.BlockSpec(memory_space=pltpu.VMEM)),
+        out_shape=jax.ShapeDtypeStruct((groups * rows, gate.shape[0] * gate.shape[2]), x.dtype),
+        in_specs=[pl.BlockSpec(memory_space=pltpu.VMEM)] * 2 + [pl.BlockSpec(memory_space=pl.ANY)] * 2,
+        out_specs=pl.BlockSpec(memory_space=pltpu.VMEM),
         scratch_shapes=[
+            pltpu.VMEM((groups * rows, parts * cols), x.dtype),
+            pltpu.VMEM((groups,) + w.shape, w.dtype),
+            pltpu.VMEM(gate.shape, gate.dtype),
+            pltpu.VMEM(up.shape, up.dtype),
             pltpu.SemaphoreType.DMA((n_send,)),
             pltpu.SemaphoreType.DMA((2, groups * parts)),
             pltpu.SemaphoreType.DMA((groups - 1,)),
             pltpu.SemaphoreType.DMA((groups,)),
             pltpu.SemaphoreType.DMA,
+            pltpu.SemaphoreType.DMA((2,)),
         ],
-        compiler_params=pltpu.CompilerParams(collective_id=0, has_side_effects=True, vmem_limit_bytes=16 << 20),
-        name="gather_tokens",
-    )(x, w)
+        compiler_params=pltpu.CompilerParams(collective_id=0, has_side_effects=True, vmem_limit_bytes=58 << 20),
+        name="gather_hidden",
+    )(x, w, gate, up)
 
 
 def scatter_kernel(sizes, p_ref, out_ref, buf_c, buf_1, buf_2, buf_z, send_sem, recv_c, recv_1, recv_2, recv_z):
@@ -195,26 +233,29 @@
                 total = total + src[at, :].astype(jnp.float32)
             dst[at, :] = total.astype(dst.dtype)
 
-    zs = list(range(1, nz)) + [0]
-    for a, b in ((1, 1), (1, 0), (0, 1), (0, 0)):
-        for d in zs:
+    zs = list(range(nz))[::-1]
+    for d in zs:
+        for a, b in ((1, 1), (1, 0), (0, 1), (0, 0)):
             for h in range(2):
                 send(local(h, rel_of(h, a, b, d) + (1,)), buf_c.at[h, a, b, d], recv_c.at[h, a, b, d], (0, 0, 0, 1))
-    for b in (1, 0):
-        for d in zs:
+
+    def step_first(d):
+        for b in (1, 0):
             for h in range(2):
                 piece = buf_c.at[h, 1, b, d]
                 arrive(piece, recv_c.at[h, 1, b, d])
                 add(piece, piece, local(h, rel_of(h, 1, b, d) + (0,)))
                 send(piece, buf_1.at[h, b, d], recv_1.at[h, b, d], first[h])
-    for d in zs:
+
+    def step_second(d):
         for h in range(2):
             piece = buf_c.at[h, 0, 1, d]
             arrive(piece, recv_c.at[h, 0, 1, d])
             arrive(buf_1.at[h, 1, d], recv_1.at[h, 1, d])
             add(piece, piece, local(h, rel_of(h, 0, 1, d) + (0,)), buf_1.at[h, 1, d])
             send(piece, buf_2.at[h, d], recv_2.at[h, d], second[h])
-    for d in zs:
+
+    def step_last(d):
         for h in range(2):
             piece = buf_c.at[h, 0, 0, d]
             arrive(piece, recv_c.at[h, 0, 0, d])
@@ -223,11 +264,19 @@
             srcs = (piece, local(h, rel_of(h, 0, 0, d) + (0,)), buf_1.at[h, 0, d], buf_2.at[h, d])
             if d:
                 add(piece, *srcs)
-                send(piece, buf_z.at[h, nz - d - 1], recv_z.at[h, nz - d - 1], (d, 0, 0, 0))
+                send(piece, buf_z.at[h, d - 1], recv_z.at[h, d - 1], (d, 0, 0, 0))
             else:
                 for k in range(nz - 1):
                     arrive(buf_z.at[h, k], recv_z.at[h, k])
                 add(out_ref.at[pl.ds(h * half, half), :], *srcs, *[buf_z.at[h, k] for k in range(nz - 1)])
+
+    for i in range(nz + 2):
+        if i < nz:
+            step_first(zs[i])
+        if 1 <= i <= nz:
+            step_second(zs[i - 1])
+        if i >= 2:
+            step_last(zs[i - 2])
     for copy in sends:
         copy.wait_send()
 
@@ -275,11 +324,11 @@
     return wanted
 
 
-def experts_dense(x, scale, gate_weight, up_weight, down_weight):
+def hidden_units(x, scale, gate_weight, up_weight):
     members, width, units = gate_weight.shape
     rows = x.shape[0]
     tile = tile_of(rows, 256)
-    hidden = pl.pallas_call(
+    return pl.pallas_call(
         hidden_kernel,
         grid=(members, rows // tile),
         out_shape=jax.ShapeDtypeStruct((rows, members * units), x.dtype),
@@ -293,19 +342,24 @@
         compiler_params=pltpu.CompilerParams(vmem_limit_bytes=40 << 20),
         name="hidden",
     )(x, scale, gate_weight, up_weight)
+
+
+def down_product(hidden, down_weight):
+    members, units, width = down_weight.shape
+    rows = hidden.shape[0]
     down = down_weight.reshape(members * units, width)
     tile_n = tile_of(width, 512)
     tile_m = tile_of(rows, 1024)
     return pl.pallas_call(
         down_kernel,
         grid=(rows // tile_m, width // tile_n),
-        out_shape=jax.ShapeDtypeStruct((rows, width), x.dtype),
+        out_shape=jax.ShapeDtypeStruct((rows, width), hidden.dtype),
         in_specs=[
             pl.BlockSpec((tile_m, members * units), lambda m, n: (m, 0)),
             pl.BlockSpec((members * units, tile_n), lambda m, n: (0, n)),
         ],
         out_specs=pl.BlockSpec((tile_m, tile_n), lambda m, n: (m, n)),
-        compiler_params=pltpu.CompilerParams(vmem_limit_bytes=24 << 20),
+        compiler_params=pltpu.CompilerParams(vmem_limit_bytes=50 << 20),
         name="down",
     )(hidden, down)
 
@@ -314,20 +368,18 @@
     groups, parts = lax.axis_size("ep"), lax.axis_size("etp")
     members = gate_weight.shape[0]
     numbers = jnp.arange(members * groups, dtype=jnp.int32)
-    share = jnp.sum(jnp.where(numbers[:, None, None] == expert_ids[None], gate_prob[None], 0.0), axis=2)
+    share = jnp.sum(jnp.where(expert_ids[:, :, None] == numbers, gate_prob[:, :, None], 0.0), axis=1)
     size = groups * parts * tokens.size * tokens.dtype.itemsize
-    kernels = groups % 2 == 0 and groups > 2 and parts == 4 and size <= VMEM_BUDGET
+    kernels = groups > 2 and groups & (groups - 1) == 0 and parts == 4 and size <= VMEM_BUDGET
     sizes = (groups // 2, 2, parts // 2, 2)
     if kernels:
-        gathered, shares = gather(sizes, tokens, share)
-    else:
-        gathered = lax.all_gather(lax.all_gather(tokens, "ep", axis=0, tiled=True), "etp", axis=1, tiled=True)
-        shares = lax.all_gather(share, "ep", axis=0)
+        hidden = gather(sizes, tokens, share, gate_weight, up_weight)
+        return scatter(sizes, down_product(hidden, down_weight))
+    gathered = lax.all_gather(lax.all_gather(tokens, "ep", axis=0, tiled=True), "etp", axis=1, tiled=True)
+    shares = lax.all_gather(share, "ep", axis=0, tiled=True)
     mine = lax.dynamic_slice_in_dim(shares, lax.axis_index("ep") * members, members, axis=1)
-    scale = jnp.transpose(mine, (1, 0, 2)).reshape(members, -1, 1)
-    partial_sum = experts_dense(gathered, scale, gate_weight, up_weight, down_weight)
-    if kernels:
-        return scatter(sizes, partial_sum)
+    hidden = hidden_units(gathered, jnp.transpose(mine)[:, :, None], gate_weight, up_weight)
+    partial_sum = down_product(hidden, down_weight)
     summed = lax.psum_scatter(partial_sum, "etp", scatter_dimension=1, tiled=True)
     return lax.psum_scatter(summed, "ep", scatter_dimension=0, tiled=True)
 

time: 154 us -> 135 us (0.88)
  the two profiles are of different devices: /device:TPU:9 before, /device:TPU:0 now
where the time goes in v2:
time: 135 us; the launch traced here: 134 us
  Pallas kernels  127 us (94%)
  local copies, waits for them, and re-layouts  6.22 us (5%)
    pallas_call x1, Pallas kernels, gather(): pl.pallas_call(functools.partial(gather_kernel, sizes), out_shape=jax.Sha...  64.4 us
    pallas_call x1, Pallas kernels, scatter(): pl.pallas_call(functools.partial(scatter_kernel, sizes), out_shape=jax.Sh...  51.1 us
    pallas_call x1, Pallas kernels, down_product(): pl.pallas_call(down_kernel, grid=(rows // tile_m, width // tile_n), out_s...  11.8 us
    unnamed x5, local copies, waits for them, and re-layouts  5.49 us

profile of v2, /device:TPU:0, one launch (start us, length us, event | category | flops | bytes accessed | tf_op | source)
XLA Modules:
  0.0 134.2 jit_solution(4753130802519986512)
XLA Ops:
  0.0 0.7 select_reduce_fusion
  0.7 0.7 copy.9.w_ref
  1.4 64.4 %gather_hidden.1.h_ref = bf16[1024,768]{1,0:T(8,128)(2,1)} custom-call(bf16[128,1024]{1,0:T(8,128)(2,1)} %x_ref.1, f32[128,16]{1,0:T(8,128)} %copy.9.w_ref, bf16[2,4096,384]{2,1,0:T(8,128)(2,1)} %gate_hbm.1, bf16[2,4096,384]{2,1,0:T(8,128)(2,1)} %up_hbm.1), custom_call_target="tpu_custom_call" | custom-call | tf_op jit(solution)/shard_map/gather_hidden/pallas_call | solution.py:173
  65.9 0.0 copy-start.1
  65.9 1.4 %copy-done.1 = bf16[1024,768]{1,0:T(8,128)(2,1)S(1)} copy-done((bf16[1024,768]{1,0:T(8,128)(2,1)S(1)}, bf16[1024,768]{1,0:T(8,128)(2,1)}, u32[]{:S(2)}) %copy-start.1) | copy-done | bytes 1572888
  67.3 11.8 %down.1.p_ref = bf16[1024,4096]{1,0:T(8,128)(2,1)} custom-call(bf16[1024,768]{1,0:T(8,128)(2,1)S(1)} %copy-done.1, bf16[768,4096]{1,0:T(8,128)(2,1)} %bitcast.1), custom_call_target="tpu_custom_call" | custom-call | tf_op jit(solution)/shard_map/down/pallas_call | solution.py:353
  79.1 0.0 copy-start
  79.1 3.4 %copy-done = bf16[1024,4096]{1,0:T(8,128)(2,1)S(1)} copy-done((bf16[1024,4096]{1,0:T(8,128)(2,1)S(1)}, bf16[1024,4096]{1,0:T(8,128)(2,1)}, u32[]{:S(2)}) %copy-start) | copy-done | bytes 8388632
  82.4 51.1 %reduce_scatter.1 = bf16[128,1024]{1,0:T(8,128)(2,1)S(1)} custom-call(bf16[1024,4096]{1,0:T(8,128)(2,1)S(1)} %copy-done), custom_call_target="tpu_custom_call" | custom-call | tf_op jit(solution)/shard_map/reduce_scatter/pallas_call | solution.py:290
  133.5 0.7 copy.11
Async XLA Ops:
  65.9 1.4 %copy-start.1 = (bf16[1024,768]{1,0:T(8,128)(2,1)S(1)}, bf16[1024,768]{1,0:T(8,128)(2,1)}, u32[]{:S(2)}) copy-start(bf16[1024,768]{1,0:T(8,128)(2,1)} %gather_hidden.1.h_ref) | copy-start | bytes 4718596
  79.1 3.4 %copy-start = (bf16[1024,4096]{1,0:T(8,128)(2,1)S(1)}, bf16[1024,4096]{1,0:T(8,128)(2,1)}, u32[]{:S(2)}) copy-start(bf16[1024,4096]{1,0:T(8,128)(2,1)} %down.1.p_ref) | copy-start | bytes 25165828
